TPU v7x, 32 devices: a whole 2x2x4 slice. The times are simulated.
32 devices in a mesh: blk: 16 (over z, y, core), team: 2 (over x).
Axes of the slice: x: 2, y: 2, z: 4, core: 2. Of those that a mesh axis runs over, the one named last changes fastest.
Arguments:
- positions: float32 [16384, 3], P('blk'), may hold values from 0 to 1
- velocity: float32 [16384, 3], P('blk'), may hold values from -6 to 6
- masses: float32 [16384], P('blk'), may hold values from 6.1035157e-06 to 0.00061035156
Outputs:
- accel: float32 [16384, 3], P('blk')
- velocity_next: float32 [16384, 3], P('blk')
- positions_next: float32 [16384, 3], P('blk')
All inputs are finite; a program needn't handle non-finite values.
Results may differ from a plain program's by a relative error of at most 0.0003.
Values sent between devices are 32-bit elements.
A program may use at most 64 MiB of HBM per device.

v0:
```python
import jax
import jax.numpy as jnp
from jax import lax
from jax.sharding import PartitionSpec as P

SOFTEN_SQ = 0.0004
TIME_STEP = 0.01


def passed_along(block, axis, distance):
    devices = range(lax.axis_size(axis))
    route = [((i - distance) % len(devices), i) for i in devices]
    return lax.ppermute(block, axis, route)


def attract(targets, sources):
    deltas = [sources[None, :, column] - targets[:, column : column + 1] for column in range(3)]
    dist_sq = deltas[0] * deltas[0] + deltas[1] * deltas[1] + deltas[2] * deltas[2] + SOFTEN_SQ
    inverse = lax.rsqrt(dist_sq)
    weight = sources[None, :, 3] * inverse * inverse * inverse
    return jnp.stack([jnp.sum(weight * delta, axis=1) for delta in deltas], axis=1)


def per_device(positions, velocity, masses):
    packed = jnp.concatenate([positions, masses[:, None]], axis=1)
    blocks = lax.axis_size("blk")
    half = blocks // 2
    member = lax.axis_index("team")
    rows = positions.shape[0]
    following = passed_along(packed, "blk", -1)
    doubled = jnp.concatenate([packed, following], axis=0)
    far = passed_along(doubled, "blk", -half)
    carried = jnp.where(member == 1, far, doubled)

    def advance_pair(counter, state):
        summed, holding = state
        summed = summed + attract(positions, holding)
        return (summed, passed_along(holding, "blk", -2))

    summed, carried = lax.fori_loop(
        0, half // 2 - 1, advance_pair, (jnp.zeros((rows, 3), jnp.float32), carried)
    )
    summed = summed + attract(positions, carried)
    accel = lax.psum(summed, "team")
    velocity_next = velocity + TIME_STEP * accel
    positions_next = positions + TIME_STEP * velocity_next
    return (accel, velocity_next, positions_next)


def solution(mesh):
    in_specs = (P("blk", None), P("blk", None), P("blk"))
    out_specs = (P("blk", None), P("blk", None), P("blk", None))
    return jax.shard_map(
        per_device, mesh=mesh, in_specs=in_specs, out_specs=out_specs, check_vma=False
    )
```

profile of v0, /device:TPU:0, one launch (start us, length us, event | category | flops | bytes accessed | tf_op | source)
XLA Modules:
  0.0 52.1 jit_solution(14040459949676174283)
XLA Ops:
  0.6 0.0 copy-start.2
  0.6 0.0 copy-start
  0.6 0.8 %pad_maximum_fusion.1 = f32[1024,4]{0,1:T(4,128)S(1)} fusion(f32[1024,1]{0,1:T(1,128)} %bitcast.51, f32[1024,3]{0,1:T(4,128)} %param.5), kind=kLoop, calls=%fused_computation.30 | loop fusion | flops 4096 | bytes 32768 | tf_op jit(solution)/shard_map/concatenate | solution.py:25
  1.4 5.6 %collective-permute-start.1 = (f32[1024,4]{0,1:T(4,128)S(1)}, f32[1024,4]{0,1:T(4,128)S(1)}, u32[]{:S(2)}, u32[]{:S(2)}) collective-permute-start(f32[1024,4]{0,1:T(4,128)S(1)} %pad_maximum_fusion.1), channel_id=1, source_target_pairs={{2,0},{4,2},{6,4},{8,6},{10,8},{12,10},{14,12},{16,14},{18,16},{20... | collective-permute-start | bytes 49160 | tf_op jit(solution)/shard_map/ppermute | solution.py:13
  7.0 1.4 %collective-permute-done.1 = f32[1024,4]{0,1:T(4,128)S(1)} collective-permute-done((f32[1024,4]{0,1:T(4,128)S(1)}, f32[1024,4]{0,1:T(4,128)S(1)}, u32[]{:S(2)}, u32[]{:S(2)}) %collective-permute-start.1) | collective-permute-done | bytes 16416 | tf_op jit(solution)/shard_map/ppermute | solution.py:13
  8.4 0.0 copy-done.2
  8.5 0.0 copy-done
  8.5 0.1 collective-permute-start.2
  8.6 4.8 %collective-permute-done.2 = f32[2048,4]{0,1:T(4,128)S(1)} collective-permute-done((f32[2048,4]{0,1:T(4,128)S(1)}, f32[2048,4]{0,1:T(4,128)S(1)}, u32[]{:S(2)}, u32[]{:S(2)}) %collective-permute-start.2) | collective-permute-done | bytes 32800 | tf_op jit(solution)/shard_map/ppermute | solution.py:13
  13.4 23.2 %while.13 = (s32[]{:T(128)}, f32[1024,3]{0,1:T(4,128)S(1)}, f32[2048,4]{0,1:T(4,128)S(1)}, f32[1024,3]{0,1:T(4,128)S(1)}, s32[]{:T(128)}, /*index=5*/s32[]{:T(128)}) while((s32[]{:T(128)}, f32[1024,3]{0,1:T(4,128)S(1)}, f32[2048,4]{0,1:T(4,128)S(1)}, f32[1024,3]{0,1:T(4,128)S(1)}, s32[]{:T(128)}, /*index=5*/s32[]{:T(128)}) %tuple.50), condition=%wide.region_4.5_spmd.clone, body=%wide.region_0.4_spmd.clone.sunk | while | flops 37757952 | bytes 381047 | solution.py:40
  13.4 0.9 %collective-permute-start = (f32[2048,4]{0,1:T(4,128)S(1)}, f32[2048,4]{0,1:T(4,128)S(1)}, u32[]{:S(2)}, u32[]{:S(2)}) collective-permute-start(f32[2048,4]{0,1:T(4,128)S(1)} %copy.11), channel_id=1, source_target_pairs={{4,0},{6,2},{8,4},{10,6},{12,8},{14,10},{16,12},{18,14},{20,16},{2... | collective-permute-start | bytes 98312 | tf_op jit(solution)/shard_map/while/body/eval_jaxpr/ppermute | solution.py:13
  14.3 6.7 %fusion.23 = (f32[1024]{0:T(1024)S(1)}, f32[1024]{0:T(1024)S(1)}, f32[1024]{0:T(1024)S(1)}) fusion(f32[1024]{0:T(1024)S(1)} %bitcast.50, f32[2048]{0:T(1024)S(1)} %bitcast.44, f32[1024]{0:T(1024)S(1)} %bitcast.49, f32[2048]{0:T(1024)S(1)} %bitcast.42, f32[1024]{0:T(1024)S(1)} %bitcast.48, f32[2048]{0:T(1024)S(1)} %bitcast.43, f32[2048]{0:T(1024)S(1)} %bitcast.41), kind=kLoop, calls=%fused_computation.11.clone.1 | loop fusion | flops 37745664 | bytes 57344 | tf_op jit(solution)/shard_map/while/body/eval_jaxpr/reduce_sum | solution.py:21
  21.0 0.0 collective-permute-done
  21.0 1.9 %collective-permute-start = (f32[2048,4]{0,1:T(4,128)S(1)}, f32[2048,4]{0,1:T(4,128)S(1)}, u32[]{:S(2)}, u32[]{:S(2)}) collective-permute-start(f32[2048,4]{0,1:T(4,128)S(1)} %copy.11), channel_id=1, source_target_pairs={{4,0},{6,2},{8,4},{10,6},{12,8},{14,10},{16,12},{18,14},{20,16},{2... | collective-permute-start | bytes 98312 | tf_op jit(solution)/shard_map/while/body/eval_jaxpr/ppermute | solution.py:13
  23.0 6.7 %fusion.23 = (f32[1024]{0:T(1024)S(1)}, f32[1024]{0:T(1024)S(1)}, f32[1024]{0:T(1024)S(1)}) fusion(f32[1024]{0:T(1024)S(1)} %bitcast.50, f32[2048]{0:T(1024)S(1)} %bitcast.44, f32[1024]{0:T(1024)S(1)} %bitcast.49, f32[2048]{0:T(1024)S(1)} %bitcast.42, f32[1024]{0:T(1024)S(1)} %bitcast.48, f32[2048]{0:T(1024)S(1)} %bitcast.43, f32[2048]{0:T(1024)S(1)} %bitcast.41), kind=kLoop, calls=%fused_computation.11.clone.1 | loop fusion | flops 37745664 | bytes 57344 | tf_op jit(solution)/shard_map/while/body/eval_jaxpr/reduce_sum | solution.py:21
  29.7 0.0 collective-permute-done
  29.7 0.1 collective-permute-start
  29.9 6.7 %fusion.23 = (f32[1024]{0:T(1024)S(1)}, f32[1024]{0:T(1024)S(1)}, f32[1024]{0:T(1024)S(1)}) fusion(f32[1024]{0:T(1024)S(1)} %bitcast.50, f32[2048]{0:T(1024)S(1)} %bitcast.44, f32[1024]{0:T(1024)S(1)} %bitcast.49, f32[2048]{0:T(1024)S(1)} %bitcast.42, f32[1024]{0:T(1024)S(1)} %bitcast.48, f32[2048]{0:T(1024)S(1)} %bitcast.43, f32[2048]{0:T(1024)S(1)} %bitcast.41), kind=kLoop, calls=%fused_computation.11.clone.1 | loop fusion | flops 37745664 | bytes 57344 | tf_op jit(solution)/shard_map/while/body/eval_jaxpr/reduce_sum | solution.py:21
  36.6 0.0 collective-permute-done
  36.6 6.7 %fusion.11 = (f32[1024]{0:T(1024)S(1)}, f32[1024]{0:T(1024)S(1)}, f32[1024]{0:T(1024)S(1)}) fusion(f32[1024]{0:T(1024)S(1)} %bitcast.59, f32[2048]{0:T(1024)S(1)} %bitcast.55, f32[1024]{0:T(1024)S(1)} %bitcast.60, f32[2048]{0:T(1024)S(1)} %bitcast.56, f32[1024]{0:T(1024)S(1)} %bitcast.58, f32[2048]{0:T(1024)S(1)} %bitcast.57, f32[2048]{0:T(1024)S(1)} %bitcast.54), kind=kLoop, calls=%fused_computation.26 | loop fusion | flops 37745664 | bytes 57344 | tf_op jit(solution)/shard_map/reduce_sum | solution.py:21
  43.3 0.0 copy-start.3
  43.3 8.1 %psum.7 = f32[1024,3]{0,1:T(4,128)S(1)} all-reduce(f32[1024,3]{0,1:T(4,128)S(1)} %maximum_add_fusion.1), channel_id=1, replica_groups=mesh['blk'=16,'team'=2] {'team'}, use_global_device_ids=true, to_apply=%region_8.9 | all-reduce | flops 3072 | bytes 24576 | tf_op jit(solution)/shard_map/psum | solution.py:44
  51.5 0.0 copy-done.3
  51.5 0.0 copy-start.1
  51.5 0.6 %multiply_add_fusion = (f32[1024,3]{0,1:T(4,128)}, f32[1024,3]{0,1:T(4,128)}) fusion(f32[1024,3]{0,1:T(4,128)S(1)} %get-tuple-element.138, f32[1024,3]{0,1:T(4,128)S(1)} %copy-done.3, f32[1024,3]{0,1:T(4,128)S(1)} %psum.7), kind=kLoop, calls=%fused_computation.32 | loop fusion | flops 12288 | bytes 61440 | tf_op jit(solution)/shard_map/add | solution.py:46
  52.1 0.0 copy-done.1
  (18 shorter events, 0.3 us)
Async XLA Ops:
  0.6 7.8 %copy-start.2 = (f32[1024]{0:T(1024)S(1)}, f32[1024]{0:T(1024)}, u32[]{:S(2)}) copy-start(f32[1024]{0:T(1024)} %param.7) | copy-start | bytes 12292
  0.6 7.8 %copy-start = (f32[1024,3]{0,1:T(4,128)S(1)}, f32[1024,3]{0,1:T(4,128)}, u32[]{:S(2)}) copy-start(f32[1024,3]{0,1:T(4,128)} %param.5) | copy-start | bytes 36868
  1.4 7.0 %collective-permute-start.1 = (f32[1024,4]{0,1:T(4,128)S(1)}, f32[1024,4]{0,1:T(4,128)S(1)}, u32[]{:S(2)}, u32[]{:S(2)}) collective-permute-start(f32[1024,4]{0,1:T(4,128)S(1)} %pad_maximum_fusion.1), channel_id=1, source_target_pairs={{2,0},{4,2},{6,4},{8,6},{10,8},{12,10},{14,12},{16,14},{18,16},{20... | collective-permute-start | bytes 49160 | tf_op jit(solution)/shard_map/ppermute | solution.py:13
  8.5 4.9 %collective-permute-start.2 = (f32[2048,4]{0,1:T(4,128)S(1)}, f32[2048,4]{0,1:T(4,128)S(1)}, u32[]{:S(2)}, u32[]{:S(2)}) collective-permute-start(f32[2048,4]{0,1:T(4,128)S(1)} %pad_maximum_fusion), channel_id=1, source_target_pairs={{16,0},{18,2},{20,4},{22,6},{24,8},{26,10},{28,12},{30,14},{0,16},... | collective-permute-start | bytes 98312 | tf_op jit(solution)/shard_map/ppermute | solution.py:13
  13.4 7.6 %collective-permute-start = (f32[2048,4]{0,1:T(4,128)S(1)}, f32[2048,4]{0,1:T(4,128)S(1)}, u32[]{:S(2)}, u32[]{:S(2)}) collective-permute-start(f32[2048,4]{0,1:T(4,128)S(1)} %copy.11), channel_id=1, source_target_pairs={{4,0},{6,2},{8,4},{10,6},{12,8},{14,10},{16,12},{18,14},{20,16},{2... | collective-permute-start | bytes 98312 | tf_op jit(solution)/shard_map/while/body/eval_jaxpr/ppermute | solution.py:13
  21.0 8.6 %collective-permute-start = (f32[2048,4]{0,1:T(4,128)S(1)}, f32[2048,4]{0,1:T(4,128)S(1)}, u32[]{:S(2)}, u32[]{:S(2)}) collective-permute-start(f32[2048,4]{0,1:T(4,128)S(1)} %copy.11), channel_id=1, source_target_pairs={{4,0},{6,2},{8,4},{10,6},{12,8},{14,10},{16,12},{18,14},{20,16},{2... | collective-permute-start | bytes 98312 | tf_op jit(solution)/shard_map/while/body/eval_jaxpr/ppermute | solution.py:13
  29.7 6.9 %collective-permute-start = (f32[2048,4]{0,1:T(4,128)S(1)}, f32[2048,4]{0,1:T(4,128)S(1)}, u32[]{:S(2)}, u32[]{:S(2)}) collective-permute-start(f32[2048,4]{0,1:T(4,128)S(1)} %copy.11), channel_id=1, source_target_pairs={{4,0},{6,2},{8,4},{10,6},{12,8},{14,10},{16,12},{18,14},{20,16},{2... | collective-permute-start | bytes 98312 | tf_op jit(solution)/shard_map/while/body/eval_jaxpr/ppermute | solution.py:13
  43.3 8.2 %copy-start.3 = (f32[1024,3]{0,1:T(4,128)S(1)}, f32[1024,3]{0,1:T(4,128)}, u32[]{:S(2)}) copy-start(f32[1024,3]{0,1:T(4,128)} %param.6) | copy-start | bytes 36868
  51.5 0.6 %copy-start.1 = (f32[1024,3]{0,1:T(4,128)}, f32[1024,3]{0,1:T(4,128)S(1)}, u32[]{:S(2)}) copy-start(f32[1024,3]{0,1:T(4,128)S(1)} %psum.7) | copy-start | bytes 36868
where the time goes:
time: 52.4 us; the launch traced here: 52.1 us
  other arithmetic  28.2 us (54%)
  starting transfers between devices  8.52 us (16%)
  blocking collectives  8.15 us (16%)
  waiting for transfers between devices  6.22 us (12%)
  between operations  0.73 us (1%)
    reduce_sum x4, other arithmetic, attract(): jnp.sum(weight * delta, axis=1)  26.6 us
    ppermute x5, starting transfers between devices, passed_along(): return lax.ppermute(block, axis, route)  8.52 us
    psum x1, blocking collectives, per_device(): accel = lax.psum(summed, 'team')  8.15 us
    ppermute x5, waiting for transfers between devices, passed_along(): return lax.ppermute(block, axis, route)  6.22 us
  transfers between devices with their start and end apart: 5, of which 2 were waited for; matrix products, arithmetic and copies ran while one was open for 39% of the time, Pallas kernels for 0%

commit v1 on v0

v1 whole, which is shorter than its diff:
```python
import functools

import jax
import jax.numpy as jnp
from jax import lax
from jax.experimental import pallas as pl
from jax.experimental.pallas import tpu as pltpu
from jax.sharding import PartitionSpec as P

SOFTEN_SQ = 0.0004
TIME_STEP = 0.01
MESH = pl.DeviceIdType.MESH
CHUNK = 256


def split3(values):
    high = values.astype(jnp.bfloat16).astype(jnp.float32)
    rest = values - high
    middle = rest.astype(jnp.bfloat16).astype(jnp.float32)
    return high, middle, rest - middle


def kernel(
    blocks, team, pos_ref, vel_ref, mass_ref, acc_out, vel_out, pos_out,
    held, feats, total, mine, theirs, send_sem, recv_sem, part_send, part_recv,
):
    me = lax.axis_index("blk")
    member = lax.axis_index("team")
    rows = pos_ref.shape[1]
    share = rows // team

    barrier = pltpu.get_barrier_semaphore()

    def greet(step, carry):
        pl.semaphore_signal(
            barrier, inc=1, device_id=(lax.rem(me + step, blocks), member), device_id_type=MESH
        )
        return carry

    lax.fori_loop(1, blocks, greet, 0)
    for step in range(1, team):
        pl.semaphore_signal(
            barrier, inc=1, device_id=(me, lax.rem(member + step, team)), device_id_type=MESH
        )

    first = pl.multiple_of(member * share, share)
    held[0, 0:3, :] = pos_ref[:, pl.ds(first, share)]
    held[0, 3:4, :] = mass_ref[:, pl.ds(first, share)]

    pos = pos_ref[...]
    centre = jnp.sum(pos, axis=1, keepdims=True) * (1.0 / rows)
    near = pos - centre
    norm = jnp.sum(near * near, axis=0, keepdims=True) + SOFTEN_SQ
    target = jnp.concatenate(
        [-2.0 * near, jnp.ones((1, rows), jnp.float32), norm, jnp.zeros((3, rows), jnp.float32)], axis=0
    )
    high, middle, low = split3(target)
    feats[...] = jnp.concatenate([high, middle, high, middle, low, high], axis=0).astype(jnp.bfloat16)
    total[...] = jnp.zeros_like(total)

    pl.semaphore_wait(barrier, blocks - 1 + team - 1)

    def passing(step):
        return pltpu.make_async_remote_copy(
            src_ref=held.at[0],
            dst_ref=held.at[step],
            send_sem=send_sem.at[step],
            recv_sem=recv_sem.at[step],
            device_id=(lax.rem(me + step, blocks), member),
            device_id_type=MESH,
        )

    def send(step, carry):
        passing(step).start()
        return carry

    lax.fori_loop(1, blocks, send, 0)

    def attract(step):
        block = held[step]
        away = block[0:3] - centre
        weight = block[3:4]
        square = jnp.sum(away * away, axis=0, keepdims=True)
        source = jnp.concatenate(
            [away, square, jnp.ones((1, share), jnp.float32), jnp.zeros((3, share), jnp.float32)], axis=0
        )
        high, middle, low = split3(source)
        left = jnp.concatenate([high, high, middle, middle, high, low], axis=0)
        left = jnp.transpose(left).astype(jnp.bfloat16)
        moment = jnp.concatenate(
            [away * weight, weight, jnp.zeros((4, share), jnp.float32)], axis=0
        )
        moments = jnp.concatenate(split3(moment), axis=0).astype(jnp.bfloat16)
        for start in range(0, rows, CHUNK):
            columns = slice(start, start + CHUNK)
            dist_sq = jnp.dot(left, feats[:, columns], preferred_element_type=jnp.float32)
            inverse = lax.rsqrt(dist_sq)
            cube = inverse * inverse * inverse
            upper = cube.astype(jnp.bfloat16)
            lower = (cube - upper.astype(jnp.float32)).astype(jnp.bfloat16)
            total[:, columns] += jnp.dot(
                moments, upper, preferred_element_type=jnp.float32
            ) + jnp.dot(moments, lower, preferred_element_type=jnp.float32)

    attract(0)

    def arrive(step, carry):
        passing(step).wait_recv()
        attract(step)
        return carry

    lax.fori_loop(1, blocks, arrive, 0)

    summed = total[0:8, :] + total[8:16, :] + total[16:24, :]
    mine[...] = summed[0:3] - near * summed[3:4]
    copies = [
        pltpu.make_async_remote_copy(
            src_ref=mine,
            dst_ref=theirs.at[step],
            send_sem=part_send.at[step],
            recv_sem=part_recv.at[step],
            device_id=(me, lax.rem(member + step, team)),
            device_id_type=MESH,
        )
        for step in range(1, team)
    ]
    for copy in copies:
        copy.start()

    def sent(step, carry):
        passing(step).wait_send()
        return carry

    lax.fori_loop(1, blocks, sent, 0)
    accel = mine[...]
    for step, copy in enumerate(copies):
        copy.wait()
        accel = accel + theirs[step + 1]
    velocity_next = vel_ref[...] + TIME_STEP * accel
    acc_out[...] = accel
    vel_out[...] = velocity_next
    pos_out[...] = pos + TIME_STEP * velocity_next


def per_device(positions, velocity, masses):
    blocks, team = lax.axis_size("blk"), lax.axis_size("team")
    rows = positions.shape[0]
    share = rows // team
    wide = jax.ShapeDtypeStruct((3, rows), jnp.float32)
    outs = pl.pallas_call(
        functools.partial(kernel, blocks, team),
        out_shape=(wide, wide, wide),
        in_specs=[pl.BlockSpec(memory_space=pltpu.VMEM)] * 3,
        out_specs=(pl.BlockSpec(memory_space=pltpu.VMEM),) * 3,
        scratch_shapes=[
            pltpu.VMEM((blocks, 4, share), jnp.float32),
            pltpu.VMEM((48, rows), jnp.bfloat16),
            pltpu.VMEM((24, rows), jnp.float32),
            pltpu.VMEM((3, rows), jnp.float32),
            pltpu.VMEM((team, 3, rows), jnp.float32),
            pltpu.SemaphoreType.DMA((blocks,)),
            pltpu.SemaphoreType.DMA((blocks,)),
            pltpu.SemaphoreType.DMA((team,)),
            pltpu.SemaphoreType.DMA((team,)),
        ],
        compiler_params=pltpu.CompilerParams(collective_id=0, has_side_effects=True),
    )(positions.T, velocity.T, masses.reshape(1, rows))
    return tuple(out.T for out in outs)


def solution(mesh):
    in_specs = (P("blk", None), P("blk", None), P("blk"))
    out_specs = (P("blk", None), P("blk", None), P("blk", None))
    return jax.shard_map(
        per_device, mesh=mesh, in_specs=in_specs, out_specs=out_specs, check_vma=False
    )
```

time: 52.4 us -> 30.6 us (0.58)
  other arithmetic: 28.2 us -> 0 us
  Pallas kernels: 0 us -> 26.8 us
  starting transfers between devices: 8.52 us -> 0 us
  blocking collectives: 8.15 us -> 0 us
  waiting for transfers between devices: 6.22 us -> 0 us
  local copies, waits for them, and re-layouts: 0.17 us -> 2.66 us
    pallas_call x0 -> x1, Pallas kernels: none -> 26.8 us  [per_device(): pl.pallas_call(functools.partial(kernel, blocks, team), out_shape=(wide,...]
    reduce_sum x4 -> x0, other arithmetic: 26.6 us -> none  [attract(): jnp.sum(weight * delta, axis=1)]
    ppermute x5 -> x0, starting transfers between devices: 8.52 us -> none  [passed_along(): return lax.ppermute(block, axis, route)]
    psum x1 -> x0, blocking collectives: 8.15 us -> none  [per_device(): accel = lax.psum(summed, 'team')]
    ppermute x5 -> x0, waiting for transfers between devices: 6.22 us -> none  [passed_along(): return lax.ppermute(block, axis, route)]
    unnamed x8 -> x7, local copies, waits for them, and re-layouts: 0.02 us -> 2.66 us
    concatenate x2 -> x0, other arithmetic: 0.81 us -> none  [the longest x1 0.79 us: per_device(): packed = jnp.concatenate([positions, masses[:, None]], axis=1)]
    add x5 -> x0, other arithmetic: 0.74 us -> none  [the longest x1 0.63 us: per_device(): positions_next = positions + TIME_STEP * velocity_next]
  transfers between devices with their start and end apart: 5 -> 0, of which waited for: 2 -> 0; matrix products, arithmetic and copies ran while one was open for 39% -> 0% of each run, Pallas kernels for 0% -> 0%
where the time goes in v1:
time: 30.6 us; the launch traced here: 30.1 us
  Pallas kernels  26.8 us (88%)
  local copies, waits for them, and re-layouts  2.66 us (9%)
  between operations  0.65 us (2%)
    pallas_call x1, Pallas kernels, per_device(): pl.pallas_call(functools.partial(kernel, blocks, team), out_shape=(wide,...  26.8 us
    unnamed x7, local copies, waits for them, and re-layouts  2.66 us

profile of v1, /device:TPU:0, one launch (start us, length us, event | category | flops | bytes accessed | tf_op | source)
XLA Modules:
  0.0 30.1 jit_solution(10080695064215814065)
XLA Ops:
  0.6 26.8 %shard_map.58 = (f32[3,1024]{1,0:T(4,128)}, f32[3,1024]{1,0:T(4,128)}, f32[3,1024]{1,0:T(4,128)}) custom-call(f32[3,1024]{1,0:T(4,128)} %bitcast.6, f32[3,1024]{1,0:T(4,128)} %bitcast.7, f32[1,1024]{1,0:T(1,128)} %bitcast.11), custom_call_target="tpu_custom_call" | custom-call | tf_op jit(solution)/shard_map/pallas_call | solution.py:150
  27.4 0.0 copy-start.1
  27.4 1.3 %copy.9 = f32[1024,3]{0,1:T(4,128)} copy(f32[1024,3]{0,1:T(4,128)} %bitcast.10) | data formatting | bytes 24576
  28.7 0.0 copy-done.1
  28.8 0.0 copy-start
  28.8 0.6 %copy.10 = f32[1024,3]{0,1:T(4,128)} copy(f32[1024,3]{0,1:T(4,128)S(1)} %bitcast.9) | data formatting | bytes 24576
  29.4 0.1 copy-done
  29.5 0.6 %copy.11 = f32[1024,3]{0,1:T(4,128)} copy(f32[1024,3]{0,1:T(4,128)S(1)} %bitcast.8) | data formatting | bytes 24576
Async XLA Ops:
  27.4 1.3 %copy-start.1 = (f32[3,1024]{1,0:T(4,128)S(1)}, f32[3,1024]{1,0:T(4,128)}, u32[]{:S(2)}) copy-start(f32[3,1024]{1,0:T(4,128)} %get-tuple-element.7) | copy-start | bytes 36868
  28.8 0.7 %copy-start = (f32[3,1024]{1,0:T(4,128)S(1)}, f32[3,1024]{1,0:T(4,128)}, u32[]{:S(2)}) copy-start(f32[3,1024]{1,0:T(4,128)} %get-tuple-element.8) | copy-start | bytes 36868
